TPU v7x, 32 devices: a whole 2x2x4 slice. The times are simulated.
32 devices in a mesh: gx: 8 (over z, y), gy: 4 (over x, core).
Axes of the slice: x: 2, y: 2, z: 4, core: 2. Of those that a mesh axis runs over, the one named last changes fastest.
Arguments:
- right_side: float32 [128, 256, 512], P('gx', 'gy'), may hold values from -8 to 8
- guess: float32 [128, 256, 512], P('gx', 'gy'), may hold values from -4 to 4
- diagonal: float32 [128, 256, 512], P('gx', 'gy'), may hold values from 0.02 to 0.5
Outputs:
- solution_field: float32 [128, 256, 512], P('gx', 'gy')
- residual: float32 [128, 256, 512], P('gx', 'gy')
All inputs are finite; a program needn't handle non-finite values.
Results may differ from a plain program's by a relative error of at most 0.00065.
Values sent between devices are 32-bit elements; how exact they have to be, the bound alone decides.
A program may use at most 128 MiB of HBM per device.

v0:
```python
import functools
import jax
import jax.numpy as jnp
from jax import lax
from jax.experimental import pallas as pl
from jax.experimental.pallas import tpu as pltpu
from jax.sharding import PartitionSpec as P

STEPS = 4
center_shift = 6.25
half_range = 6.25
PAD = 8
MESH = pl.DeviceIdType.MESH


def change_matrix(depth):
    rows = []
    for i in range(depth + 1):
        line = []
        for k in range(depth + 1):
            value = 0.0
            if k == 0:
                value = center_shift if i == 0 else half_range if i == 1 else 0.0
            elif k < depth:
                if i == k:
                    value = center_shift
                elif i == k - 1 or i == k + 1:
                    value = half_range / 2.0
            line.append(value)
        rows.append(line)
    return rows


def total(terms):
    terms = list(terms)
    while len(terms) > 1:
        pairs = [a + b for a, b in zip(terms[::2], terms[1::2])]
        terms = pairs + ([terms[-1]] if len(terms) % 2 else [])
    return terms[0]


def quad(left, gram, right):
    return total(l * total(g * r for g, r in zip(line, right)) for l, line in zip(left, gram))


def coefficient_steps(gram, depth, zero, one):
    change = change_matrix(depth)
    unit = [one] + [zero] * depth
    xc, rc, pc = [zero] * (depth + 1), unit, unit
    rr = quad(rc, gram, rc)
    for step in range(depth):
        moved = []
        for line in change:
            terms = [c * p for c, p in zip(line, pc) if c != 0.0]
            moved.append(total(terms))
        alpha = rr / quad(pc, gram, moved)
        xc = [x + alpha * p for x, p in zip(xc, pc)]
        rc = [r - alpha * m for r, m in zip(rc, moved)]
        new = quad(rc, gram, rc)
        beta = new / rr
        pc = [r + beta * p for r, p in zip(rc, pc)]
        rr = new
    return xc, rc


def fold(p):
    rows, cols = p.shape
    return total(
        p[i : i + 8, j : j + 128] for i in range(0, rows, 8) for j in range(0, cols, 128)
    )


def kernel(px, py, rows, r_hbm, g_hbm, d_hbm, sol_hbm, res_hbm,
           F, R, D, Ys, Yr, A, M1, M2, acc,
           edge_sem, load_sem, xs_sem, xr_sem, ys_sem, yr_sem, as_sem, a1_sem, a2_sem):
    ZC, LX, LY, _ = R.shape
    NC = LY // rows
    gx, gy = lax.axis_index("gx"), lax.axis_index("gy")
    low_x, high_x, low_y, high_y = gx > 0, gx < px - 1, gy > 0, gy < py - 1
    inner = pl.ds(PAD, LY)

    def column(z):
        return pl.ds(z * 128, 128)

    edges, loads = [], []
    for z in range(ZC):
        for i, x in enumerate((0, LX - 1)):
            edges.append(pltpu.make_async_copy(
                g_hbm.at[x, :, column(z)], F.at[0, z, x + 1, inner, :], edge_sem.at[z, i]))
    for z in range(ZC):
        loads.append(pltpu.make_async_copy(
            g_hbm.at[pl.ds(1, LX - 2), :, column(z)],
            F.at[0, z, pl.ds(2, LX - 2), inner, :], load_sem.at[0, z]))
    for i, (src, dst) in enumerate(((d_hbm, D), (r_hbm, R))):
        for z in range(ZC):
            loads.append(pltpu.make_async_copy(
                src.at[:, :, column(z)], dst.at[z], load_sem.at[1 + i, z]))
    for copy in edges + loads:
        copy.start()

    barrier = pltpu.get_barrier_semaphore()
    for o in range(1, px):
        pl.semaphore_signal(barrier, inc=1, device_id={"gx": lax.rem(gx + o, px)}, device_id_type=MESH)
    for o in range(1, py):
        pl.semaphore_signal(barrier, inc=1, device_id={"gy": lax.rem(gy + o, py)}, device_id_type=MESH)

    def zero_planes(x):
        def one(j, carry):
            at = pl.multiple_of(PAD + j * 8, 8)
            for k in range(STEPS + 1):
                for z in range(ZC):
                    F[k, z, x, pl.ds(at, 8), :] = jnp.zeros((8, 128), jnp.float32)
            return carry
        lax.fori_loop(0, LY // 8, one, 0)

    pl.when(jnp.logical_not(low_x))(lambda: zero_planes(0))
    pl.when(jnp.logical_not(high_x))(lambda: zero_planes(LX + 1))

    def zero_rows(side):
        for k in range(STEPS + 1):
            Yr[k, side] = jnp.zeros((ZC, LX, 128), jnp.float32)

    pl.when(jnp.logical_not(low_y))(lambda: zero_rows(0))
    pl.when(jnp.logical_not(high_y))(lambda: zero_rows(1))

    pl.semaphore_wait(barrier, px + py - 2)

    def x_copy(k, side, j):
        at = pl.ds(PAD + j * rows, rows)
        return pltpu.make_async_remote_copy(
            src_ref=F.at[k, :, 1 if side == 0 else LX, at, :],
            dst_ref=F.at[k, :, LX + 1 if side == 0 else 0, at, :],
            send_sem=xs_sem.at[k, side, j],
            recv_sem=xr_sem.at[k, side, j],
            device_id={"gx": gx - 1 if side == 0 else gx + 1},
            device_id_type=MESH,
        )

    def y_copy(k, side):
        return pltpu.make_async_remote_copy(
            src_ref=Ys.at[k, side],
            dst_ref=Yr.at[k, 1 - side],
            send_sem=ys_sem.at[k, side],
            recv_sem=yr_sem.at[k, side],
            device_id={"gy": gy - 1 if side == 0 else gy + 1},
            device_id_type=MESH,
        )

    x_has, y_has = (low_x, high_x), (low_y, high_y)

    def send_x(k, j):
        for side in (0, 1):
            pl.when(x_has[side])(lambda: x_copy(k, side, j).start())

    def wait_x(k, j):
        for side in (0, 1):
            pl.when(x_has[1 - side])(lambda: x_copy(k, side, j).wait_recv())

    def send_y(k):
        for x in range(LX):
            for z in range(ZC):
                Ys[k, 0, z, x : x + 1, :] = F[k, z, x + 1, PAD : PAD + 1, :]
                Ys[k, 1, z, x : x + 1, :] = F[k, z, x + 1, PAD + LY - 1 : PAD + LY, :]
        for side in (0, 1):
            pl.when(y_has[side])(lambda: y_copy(k, side).start())

    def wait_y(k):
        for side in (0, 1):
            pl.when(y_has[1 - side])(lambda: y_copy(k, side).wait_recv())
        for x in range(LX):
            for z in range(ZC):
                F[k, z, x + 1, PAD - 1 : PAD, :] = Yr[k, 0, z, x : x + 1, :]
                F[k, z, x + 1, PAD + LY : PAD + LY + 1, :] = Yr[k, 1, z, x : x + 1, :]

    order = [0] + ([NC - 1] if NC > 1 else []) + list(range(1, NC - 1))
    for copy in edges:
        copy.wait()
    for j in order:
        send_x(0, j)

    acc[...] = jnp.zeros(acc.shape, jnp.float32)
    zero_tile = jnp.zeros((8, 128), jnp.float32)

    c_scale = 2.0 / half_range

    def block(k, x, y, n):
        at, up, down = pl.ds(PAD + y, n), pl.ds(PAD + y + 1, n), pl.ds(PAD + y - 1, n)
        lane = lax.broadcasted_iota(jnp.int32, (n, 128), 1)
        first_lane, last_lane = lane == 0, lane == 127
        here = [F[k - 1, z, x, at, :] for z in range(ZC)]
        right = [pltpu.roll(h, 1, 1) for h in here]
        left = [pltpu.roll(h, 127, 1) for h in here]
        squares, crosses = [], []
        for z in range(ZC):
            beside = F[k - 1, z, x + 1, at, :] + F[k - 1, z, x - 1, at, :]
            beside = beside + (F[k - 1, z, x, up, :] + F[k - 1, z, x, down, :])
            before = jnp.where(first_lane, right[z - 1] if z > 0 else 0.0, right[z])
            after = jnp.where(last_lane, left[z + 1] if z < ZC - 1 else 0.0, left[z])
            beside = beside + (before + after)
            diag = D[z, x - 1, pl.ds(y, n), :]
            if k == 1:
                new = R[z, x - 1, pl.ds(y, n), :] - ((6.0 + diag) * here[z] - beside)
                D[z, x - 1, pl.ds(y, n), :] = (diag + (6.0 - center_shift)) * c_scale
            elif k == 2:
                new = (diag * here[z] - beside * c_scale) * 0.5
            else:
                new = diag * here[z] - beside * c_scale - F[k - 2, z, x, at, :]
            F[k, z, x, at, :] = new
            squares.append(fold(new * new))
            if k > 1:
                crosses.append(fold(new * here[z]))
        return total(squares), (total(crosses) if k > 1 else zero_tile)

    def add(a, b):
        return a[0] + b[0], a[1] + b[1]

    for copy in loads[:ZC]:
        copy.wait()
    send_y(0)
    for copy in loads[ZC:]:
        copy.wait()

    for k in range(1, STEPS + 2):
        sums = (zero_tile, zero_tile)
        wait_y(k - 1)
        for i, j in enumerate(order):
            wait_x(k - 1, j)
            for x in (1, LX):
                sums = add(sums, block(k, x, j * rows, rows))
            if k <= STEPS:
                send_x(k, j)
            if i == 1 and k <= STEPS:
                send_y(k)
            if i == 0:
                spans = [(0, 8), (LY - 8, 8)]
            elif i < NC - 1:
                spans = [(8 + (i - 1) * rows, rows)]
            else:
                spans = [(8 + (i - 1) * rows, LY - 16 - (i - 1) * rows)]

            def plane(x, s):
                for y, n in spans:
                    s = add(s, block(k, x, y, n))
                return s

            sums = lax.fori_loop(2, LX, plane, sums, unroll=7 if (LX - 2) % 7 == 0 else 2)
        acc[2 * (k - 1)] = sums[0]
        if k > 1:
            acc[2 * (k - 1) - 1] = sums[1]

    lane = lax.broadcasted_iota(jnp.int32, (1, 128), 1)
    row = jnp.zeros((1, 128), jnp.float32)
    count = 2 * STEPS + 1
    for m in range(count):
        s = jnp.sum(jnp.sum(acc[m], axis=0, keepdims=True), axis=1, keepdims=True)
        row = row + jnp.where(lane == m, s, 0.0)

    def exchange(stage, axis, me, peers, slots, sems, row):
        A[stage] = row
        copies = [
            pltpu.make_async_remote_copy(
                src_ref=A.at[stage], dst_ref=slots.at[o - 1],
                send_sem=as_sem.at[stage, o - 1], recv_sem=sems.at[o - 1],
                device_id={axis: lax.rem(me + o, peers)}, device_id_type=MESH,
            )
            for o in range(1, peers)
        ]
        for copy in copies:
            copy.start()
        for copy in copies:
            copy.wait_recv()
        row = total([row] + [slots[o] for o in range(peers - 1)])
        return row, copies

    row, first = exchange(0, "gy", gy, py, M1, a1_sem, row)
    row, second = exchange(1, "gx", gx, px, M2, a2_sem, row)

    got = [
        jnp.broadcast_to(jnp.sum(jnp.where(lane == m, row, 0.0), axis=1, keepdims=True), (8, 128))
        for m in range(count)
    ]
    moments = []
    for m in range(count):
        moments.append(got[m] if m < 2 else 2.0 * got[m] - got[m % 2])
    gram = [
        [0.5 * (moments[i + j] + moments[abs(i - j)]) for j in range(STEPS + 1)]
        for i in range(STEPS + 1)
    ]
    xc, rc = coefficient_steps(gram, STEPS, jnp.zeros((8, 128), jnp.float32), jnp.ones((8, 128), jnp.float32))

    def plane(x, carry):
        for i in range(LY // 8):
            at, to = pl.ds(PAD + i * 8, 8), pl.ds(i * 8, 8)
            for z in range(ZC):
                basis = [F[k + 1, z, x + 1, at, :] for k in range(STEPS + 1)]
                sol = F[0, z, x + 1, at, :]
                res = rc[0] * basis[0]
                for k in range(STEPS + 1):
                    sol = sol + xc[k] * basis[k]
                    if k > 0:
                        res = res + rc[k] * basis[k]
                sol_hbm[x, to, column(z)] = sol
                res_hbm[x, to, column(z)] = res
        return carry

    lax.fori_loop(0, LX, plane, 0)

    for k in range(STEPS + 1):
        for side in (0, 1):
            def done():
                for j in range(NC):
                    x_copy(k, side, j).wait_send()
            pl.when(x_has[side])(done)
            pl.when(y_has[side])(lambda: y_copy(k, side).wait_send())
    for copy in first + second:
        copy.wait_send()


def solution(mesh):
    px, py = mesh.shape["gx"], mesh.shape["gy"]

    def shards(right_side, guess, diagonal):
        LX, LY, LZ = guess.shape
        rows = 16
        NC, ZC = LY // rows, LZ // 128
        n = STEPS + 1
        dma = pltpu.SemaphoreType.DMA
        like = jax.ShapeDtypeStruct(guess.shape, jnp.float32)
        return pl.pallas_call(
            functools.partial(kernel, px, py, rows),
            out_shape=(like, like),
            in_specs=[pl.BlockSpec(memory_space=pl.ANY)] * 3,
            out_specs=(pl.BlockSpec(memory_space=pltpu.VMEM),) * 2,
            scratch_shapes=[
                pltpu.VMEM((n + 1, ZC, LX + 2, LY + 3 * PAD, 128), jnp.float32),
                pltpu.VMEM((ZC, LX, LY, 128), jnp.float32),
                pltpu.VMEM((ZC, LX, LY, 128), jnp.float32),
                pltpu.VMEM((n, 2, ZC, LX, 128), jnp.float32),
                pltpu.VMEM((n, 2, ZC, LX, 128), jnp.float32),
                pltpu.VMEM((2, 1, 128), jnp.float32),
                pltpu.VMEM((py - 1, 1, 128), jnp.float32),
                pltpu.VMEM((px - 1, 1, 128), jnp.float32),
                pltpu.VMEM((2 * STEPS + 1, 8, 128), jnp.float32),
                dma((ZC, 2)), dma((3, ZC)), dma((n, 2, NC)), dma((n, 2, NC)), dma((n, 2)), dma((n, 2)),
                dma((2, max(px, py) - 1)), dma((py - 1,)), dma((px - 1,)),
            ],
            compiler_params=pltpu.CompilerParams(
                collective_id=0, has_side_effects=True, vmem_limit_bytes=48 * 1024 * 1024
            ),
        )(right_side, guess, diagonal)

    spec = P("gx", "gy", None)
    return jax.shard_map(
        shards, mesh=mesh, in_specs=(spec,) * 3, out_specs=(spec,) * 2, check_vma=False
    )
```

profile of v0, /device:TPU:0, one launch (start us, length us, event | category | flops | bytes accessed | tf_op | source)
XLA Modules:
  0.0 50.1 jit_solution(4451713092957946832)
XLA Ops:
  0.6 46.8 %shard_map.50 = (f32[16,64,512]{2,1,0:T(8,128)S(1)}, f32[16,64,512]{2,1,0:T(8,128)S(1)}) custom-call(f32[16,64,512]{2,1,0:T(8,128)} %r_hbm.1, f32[16,64,512]{2,1,0:T(8,128)} %g_hbm.1, f32[16,64,512]{2,1,0:T(8,128)} %d_hbm.1), custom_call_target="tpu_custom_call" | custom-call | tf_op jit(solution)/shard_map/pallas_call | solution.py:329
  47.4 1.3 %copy.7 = f32[16,64,512]{2,1,0:T(8,128)} copy(f32[16,64,512]{2,1,0:T(8,128)S(1)} %get-tuple-element.4) | data formatting | bytes 4194304
  48.8 1.3 %copy.8 = f32[16,64,512]{2,1,0:T(8,128)} copy(f32[16,64,512]{2,1,0:T(8,128)S(1)} %get-tuple-element.5) | data formatting | bytes 4194304
where the time goes:
time: 50.2 us; the launch traced here: 50.1 us
  Pallas kernels  46.8 us (93%)
  local copies, waits for them, and re-layouts  2.64 us (5%)
  between operations  0.64 us (1%)
    pallas_call x1, Pallas kernels, shards(): pl.pallas_call(functools.partial(kernel, px, py, rows), out_shape=(like,...  46.8 us
    unnamed x2, local copies, waits for them, and re-layouts  2.64 us

commit v1 on v0

--- a/solution.py
+++ b/solution.py
@@ -43,16 +43,18 @@
     return total(l * total(g * r for g, r in zip(line, right)) for l, line in zip(left, gram))
 
 
+def moved_by(change, pc):
+    lines = [[c * p for c, p in zip(line, pc) if c != 0.0] for line in change]
+    return [total(terms) for terms in lines]
+
+
 def coefficient_steps(gram, depth, zero, one):
-    change = change_matrix(depth)
-    unit = [one] + [zero] * depth
-    xc, rc, pc = [zero] * (depth + 1), unit, unit
+    change = [line[:depth] for line in change_matrix(depth)]
+    unit = [one] + [zero] * (depth - 1)
+    xc, rc, pc = [zero] * depth, unit, unit
     rr = quad(rc, gram, rc)
-    for step in range(depth):
-        moved = []
-        for line in change:
-            terms = [c * p for c, p in zip(line, pc) if c != 0.0]
-            moved.append(total(terms))
+    for step in range(depth - 1):
+        moved = moved_by(change[:depth], pc)
         alpha = rr / quad(pc, gram, moved)
         xc = [x + alpha * p for x, p in zip(xc, pc)]
         rc = [r - alpha * m for r, m in zip(rc, moved)]
@@ -60,7 +62,22 @@
         beta = new / rr
         pc = [r + beta * p for r, p in zip(rc, pc)]
         rr = new
-    return xc, rc
+    moved = moved_by(change, pc)
+    return xc + [zero], rc + [zero], pc + [zero], moved, rr
+
+
+def gram_of(moments, size):
+    return [
+        [0.5 * (moments[i + j] + moments[abs(i - j)]) for j in range(size)] for i in range(size)
+    ]
+
+
+def reach(count, known):
+    steps = []
+    while known < count - 1:
+        steps.append(max(known, 1))
+        known += steps[-1]
+    return steps
 
 
 def fold(p):
@@ -70,9 +87,9 @@
     )
 
 
-def kernel(px, py, rows, r_hbm, g_hbm, d_hbm, sol_hbm, res_hbm,
-           F, R, D, Ys, Yr, A, M1, M2, acc,
-           edge_sem, load_sem, xs_sem, xr_sem, ys_sem, yr_sem, as_sem, a1_sem, a2_sem):
+def kernel(px, py, rows, r_hbm, g_hbm, d_hbm, sol_out, step_out, res_out, moved_out, alpha_out,
+           F, R, D, Ys, Yr, A, M, acc,
+           edge_sem, load_sem, xs_sem, xr_sem, ys_sem, yr_sem, as_sem, ar_sem, met_sem):
     ZC, LX, LY, _ = R.shape
     NC = LY // rows
     gx, gy = lax.axis_index("gx"), lax.axis_index("gy")
@@ -98,11 +115,22 @@
     for copy in edges + loads:
         copy.start()
 
+    x_has, y_has = (low_x, high_x), (low_y, high_y)
+
+    def partners(axis, distance):
+        me, count = (gx, px) if axis == "gx" else (gy, py)
+        return [(me >= distance, {axis: me - distance}), (me < count - distance, {axis: me + distance})]
+
+    def greet(sem, pairs):
+        for there, device in pairs:
+            pl.when(there)(lambda: pl.semaphore_signal(sem, inc=1, device_id=device, device_id_type=MESH))
+
+    def meet(sem, pairs):
+        pl.semaphore_wait(sem, sum(there.astype(jnp.int32) for there, _ in pairs))
+
     barrier = pltpu.get_barrier_semaphore()
-    for o in range(1, px):
-        pl.semaphore_signal(barrier, inc=1, device_id={"gx": lax.rem(gx + o, px)}, device_id_type=MESH)
-    for o in range(1, py):
-        pl.semaphore_signal(barrier, inc=1, device_id={"gy": lax.rem(gy + o, py)}, device_id_type=MESH)
+    beside = partners("gx", 1) + partners("gy", 1)
+    greet(barrier, beside)
 
     def zero_planes(x):
         def one(j, carry):
@@ -123,7 +151,44 @@
     pl.when(jnp.logical_not(low_y))(lambda: zero_rows(0))
     pl.when(jnp.logical_not(high_y))(lambda: zero_rows(1))
 
-    pl.semaphore_wait(barrier, px + py - 2)
+    meet(barrier, beside)
+
+    meetings = [("gx", o) for o in reach(px, 1)] + [("gy", o) for o in reach(py, 0)]
+    met = []
+
+    def spread(last=False):
+        while len(met) <= len(meetings):
+            n = len(met)
+            if n > 0:
+                meet(met_sem.at[n - 1], partners(*meetings[n - 1]))
+            if n < len(meetings):
+                greet(met_sem.at[n], partners(*meetings[n]))
+            met.append(n)
+            if not last:
+                break
+
+    me = gx * py + gy
+
+    def send_sums(stage, row):
+        A[stage] = row
+        M[stage, me] = row
+        for ox in range(px):
+            for oy in range(py):
+                if ox or oy:
+                    pltpu.make_async_remote_copy(
+                        src_ref=A.at[stage], dst_ref=M.at[stage, me],
+                        send_sem=as_sem.at[stage], recv_sem=ar_sem.at[stage],
+                        device_id={"gx": lax.rem(gx + ox, px), "gy": lax.rem(gy + oy, py)},
+                        device_id_type=MESH,
+                    ).start()
+
+    def all_sums(stage):
+        peers = pl.ds(0, px * py - 1)
+        return pltpu.make_async_remote_copy(
+            src_ref=M.at[stage, peers], dst_ref=M.at[stage, peers],
+            send_sem=as_sem.at[stage], recv_sem=ar_sem.at[stage],
+            device_id={"gx": lax.rem(gx + 1, px)}, device_id_type=MESH,
+        )
 
     def x_copy(k, side, j):
         at = pl.ds(PAD + j * rows, rows)
@@ -145,8 +210,6 @@
             device_id={"gy": gy - 1 if side == 0 else gy + 1},
             device_id_type=MESH,
         )
-
-    x_has, y_has = (low_x, high_x), (low_y, high_y)
 
     def send_x(k, j):
         for side in (0, 1):
@@ -220,16 +283,32 @@
     for copy in loads[ZC:]:
         copy.wait()
 
-    for k in range(1, STEPS + 2):
+    lane = lax.broadcasted_iota(jnp.int32, (1, 128), 1)
+
+    def row_of(sums):
+        row = jnp.zeros((1, 128), jnp.float32)
+        for m, part in sums:
+            s = jnp.sum(jnp.sum(part, axis=0, keepdims=True), axis=1, keepdims=True)
+            row = row + jnp.where(lane == m, s, 0.0)
+        return row
+
+    def moments_of(stage, which):
+        all_sums(stage).wait_recv()
+        row = total(M[stage, i] for i in range(px * py))
+        return {
+            m: jnp.broadcast_to(jnp.sum(jnp.where(lane == m, row, 0.0), axis=1, keepdims=True), (8, 128))
+            for m in which
+        }
+
+    for k in range(1, STEPS + 1):
         sums = (zero_tile, zero_tile)
         wait_y(k - 1)
         for i, j in enumerate(order):
             wait_x(k - 1, j)
             for x in (1, LX):
                 sums = add(sums, block(k, x, j * rows, rows))
-            if k <= STEPS:
-                send_x(k, j)
-            if i == 1 and k <= STEPS:
+            send_x(k, j)
+            if i == 1:
                 send_y(k)
             if i == 0:
                 spans = [(0, 8), (LY - 8, 8)]
@@ -244,49 +323,39 @@
                 return s
 
             sums = lax.fori_loop(2, LX, plane, sums, unroll=7 if (LX - 2) % 7 == 0 else 2)
+            if i % 2 == 0:
+                spread()
         acc[2 * (k - 1)] = sums[0]
         if k > 1:
             acc[2 * (k - 1) - 1] = sums[1]
 
-    lane = lax.broadcasted_iota(jnp.int32, (1, 128), 1)
-    row = jnp.zeros((1, 128), jnp.float32)
-    count = 2 * STEPS + 1
-    for m in range(count):
-        s = jnp.sum(jnp.sum(acc[m], axis=0, keepdims=True), axis=1, keepdims=True)
-        row = row + jnp.where(lane == m, s, 0.0)
-
-    def exchange(stage, axis, me, peers, slots, sems, row):
-        A[stage] = row
-        copies = [
-            pltpu.make_async_remote_copy(
-                src_ref=A.at[stage], dst_ref=slots.at[o - 1],
-                send_sem=as_sem.at[stage, o - 1], recv_sem=sems.at[o - 1],
-                device_id={axis: lax.rem(me + o, peers)}, device_id_type=MESH,
-            )
-            for o in range(1, peers)
-        ]
-        for copy in copies:
-            copy.start()
-        for copy in copies:
-            copy.wait_recv()
-        row = total([row] + [slots[o] for o in range(peers - 1)])
-        return row, copies
-
-    row, first = exchange(0, "gy", gy, py, M1, a1_sem, row)
-    row, second = exchange(1, "gx", gx, px, M2, a2_sem, row)
-
-    got = [
-        jnp.broadcast_to(jnp.sum(jnp.where(lane == m, row, 0.0), axis=1, keepdims=True), (8, 128))
-        for m in range(count)
-    ]
-    moments = []
-    for m in range(count):
-        moments.append(got[m] if m < 2 else 2.0 * got[m] - got[m % 2])
-    gram = [
-        [0.5 * (moments[i + j] + moments[abs(i - j)]) for j in range(STEPS + 1)]
-        for i in range(STEPS + 1)
-    ]
-    xc, rc = coefficient_steps(gram, STEPS, jnp.zeros((8, 128), jnp.float32), jnp.ones((8, 128), jnp.float32))
+    spread(last=True)
+    early, late = range(2 * STEPS - 1), range(2 * STEPS - 1, 2 * STEPS + 1)
+    send_sums(0, row_of([(m, acc[m]) for m in early]))
+
+    last = STEPS + 1
+    wait_y(last - 1)
+
+    def inner_plane(x, s):
+        for y in range(0, LY, rows):
+            s = add(s, block(last, x, y, rows))
+        return s
+
+    sums = lax.fori_loop(2, LX, inner_plane, (zero_tile, zero_tile))
+    for j in order:
+        wait_x(last - 1, j)
+        for x in (1, LX):
+            sums = add(sums, block(last, x, j * rows, rows))
+    send_sums(1, row_of([(2 * STEPS - 1, sums[1]), (2 * STEPS, sums[0])]))
+
+    got = moments_of(0, early)
+
+    def moment(m):
+        return got[m] if m < 2 else 2.0 * got[m] - got[m % 2]
+
+    moments = [moment(m) for m in early]
+    zero, one = jnp.zeros((8, 128), jnp.float32), jnp.ones((8, 128), jnp.float32)
+    xc, rc, pc, moved, rr = coefficient_steps(gram_of(moments, STEPS), STEPS, zero, one)
 
     def plane(x, carry):
         for i in range(LY // 8):
@@ -294,16 +363,18 @@
             for z in range(ZC):
                 basis = [F[k + 1, z, x + 1, at, :] for k in range(STEPS + 1)]
                 sol = F[0, z, x + 1, at, :]
-                res = rc[0] * basis[0]
                 for k in range(STEPS + 1):
                     sol = sol + xc[k] * basis[k]
-                    if k > 0:
-                        res = res + rc[k] * basis[k]
-                sol_hbm[x, to, column(z)] = sol
-                res_hbm[x, to, column(z)] = res
+                sol_out[x, to, column(z)] = sol
+                for out, coefficients in ((step_out, pc), (res_out, rc), (moved_out, moved)):
+                    out[x, to, column(z)] = total(c * b for c, b in zip(coefficients, basis))
         return carry
 
     lax.fori_loop(0, LX, plane, 0)
+
+    got.update(moments_of(1, late))
+    moments += [moment(m) for m in late]
+    alpha_out[...] = rr / quad(pc, gram_of(moments, STEPS + 1), moved)
 
     for k in range(STEPS + 1):
         for side in (0, 1):
@@ -312,8 +383,29 @@
                     x_copy(k, side, j).wait_send()
             pl.when(x_has[side])(done)
             pl.when(y_has[side])(lambda: y_copy(k, side).wait_send())
-    for copy in first + second:
-        copy.wait_send()
+    for stage in (0, 1):
+        all_sums(stage).wait_send()
+
+
+def last_step(sol_ref, step_ref, res_ref, moved_ref, alpha_ref, sol_hbm, res_hbm, sol, res, sems):
+    LX, LY, LZ = sol.shape
+    alpha = jnp.concatenate([alpha_ref[...]] * (LZ // 128), axis=1)
+    n = 2 if LX % 2 == 0 else 1
+    copies = []
+    for x in range(0, LX, n):
+        for i, (out, hbm) in enumerate(((sol, sol_hbm), (res, res_hbm))):
+            for p in range(x, x + n):
+                for y in range(0, LY, 8):
+                    at = (p, pl.ds(y, 8), slice(None))
+                    if i == 0:
+                        out[at] = sol_ref[at] + alpha * step_ref[at]
+                    else:
+                        out[at] = res_ref[at] - alpha * moved_ref[at]
+            planes = pl.ds(x, n)
+            copies.append(pltpu.make_async_copy(out.at[planes], hbm.at[planes], sems.at[i, x // n]))
+            copies[-1].start()
+    for copy in copies:
+        copy.wait()
 
 
 def solution(mesh):
@@ -326,11 +418,12 @@
         n = STEPS + 1
         dma = pltpu.SemaphoreType.DMA
         like = jax.ShapeDtypeStruct(guess.shape, jnp.float32)
-        return pl.pallas_call(
+        vmem, hbm = pl.BlockSpec(memory_space=pltpu.VMEM), pl.BlockSpec(memory_space=pltpu.MemorySpace.HBM)
+        parts = pl.pallas_call(
             functools.partial(kernel, px, py, rows),
-            out_shape=(like, like),
-            in_specs=[pl.BlockSpec(memory_space=pl.ANY)] * 3,
-            out_specs=(pl.BlockSpec(memory_space=pltpu.VMEM),) * 2,
+            out_shape=(like,) * 4 + (jax.ShapeDtypeStruct((8, 128), jnp.float32),),
+            in_specs=[hbm] * 3,
+            out_specs=(vmem,) * 5,
             scratch_shapes=[
                 pltpu.VMEM((n + 1, ZC, LX + 2, LY + 3 * PAD, 128), jnp.float32),
                 pltpu.VMEM((ZC, LX, LY, 128), jnp.float32),
@@ -338,16 +431,24 @@
                 pltpu.VMEM((n, 2, ZC, LX, 128), jnp.float32),
                 pltpu.VMEM((n, 2, ZC, LX, 128), jnp.float32),
                 pltpu.VMEM((2, 1, 128), jnp.float32),
-                pltpu.VMEM((py - 1, 1, 128), jnp.float32),
-                pltpu.VMEM((px - 1, 1, 128), jnp.float32),
+                pltpu.VMEM((2, px * py, 1, 128), jnp.float32),
                 pltpu.VMEM((2 * STEPS + 1, 8, 128), jnp.float32),
                 dma((ZC, 2)), dma((3, ZC)), dma((n, 2, NC)), dma((n, 2, NC)), dma((n, 2)), dma((n, 2)),
-                dma((2, max(px, py) - 1)), dma((py - 1,)), dma((px - 1,)),
+                dma((2,)), dma((2,)),
+                pltpu.SemaphoreType.REGULAR((len(reach(px, 1)) + len(reach(py, 0)),)),
             ],
             compiler_params=pltpu.CompilerParams(
-                collective_id=0, has_side_effects=True, vmem_limit_bytes=48 * 1024 * 1024
+                collective_id=0, has_side_effects=True, vmem_limit_bytes=44 * 1024 * 1024
             ),
         )(right_side, guess, diagonal)
+        return pl.pallas_call(
+            last_step,
+            out_shape=(like,) * 2,
+            in_specs=[vmem] * 5,
+            out_specs=(hbm,) * 2,
+            scratch_shapes=[pltpu.VMEM(guess.shape, jnp.float32)] * 2 + [dma((2, LX))],
+            compiler_params=pltpu.CompilerParams(vmem_limit_bytes=40 * 1024 * 1024),
+        )(*parts)
 
     spec = P("gx", "gy", None)
     return jax.shard_map(

time: 50.2 us -> 44.5 us (0.89)
  Pallas kernels: 46.8 us -> 43.8 us
  local copies, waits for them, and re-layouts: 2.64 us -> 0 us
    pallas_call x1 -> x2, Pallas kernels: 46.8 us -> 43.8 us  [the longest x1 41.4 us: shards(): pl.pallas_call(functools.partial(kernel, px, py, rows), out_shape=(like,)...]
    unnamed x2 -> x0, local copies, waits for them, and re-layouts: 2.64 us -> none
where the time goes in v1:
time: 44.5 us; the launch traced here: 44.4 us
  Pallas kernels  43.8 us (98%)
  between operations  0.64 us (1%)
    pallas_call x1, Pallas kernels, shards(): pl.pallas_call(functools.partial(kernel, px, py, rows), out_shape=(like,)...  41.4 us
    pallas_call x1, Pallas kernels, shards(): pl.pallas_call(last_step, out_shape=(like,) * 2, in_specs=[vmem] * 5, out...  2.31 us

profile of v1, /device:TPU:0, one launch (start us, length us, event | category | flops | bytes accessed | tf_op | source)
XLA Modules:
  0.0 44.4 jit_solution(761192755183806400)
XLA Ops:
  0.6 41.4 %shard_map.50 = (f32[16,64,512]{2,1,0:T(8,128)S(1)}, f32[16,64,512]{2,1,0:T(8,128)S(1)}, f32[16,64,512]{2,1,0:T(8,128)S(1)}, f32[16,64,512]{2,1,0:T(8,128)S(1)}, f32[8,128]{1,0:T(8,128)S(1)}) custom-call(f32[16,64,512]{2,1,0:T(8,128)} %r_hbm.1, f32[16,64,512]{2,1,0:T(8,128)} %g_hbm.1, f32[16,64,512]{2,1,0:T(8,128)} %d_hbm.1), custom_call_target="tpu_custom_call" | custom-call | tf_op jit(solution)/shard_map/pallas_call | solution.py:422
  42.1 2.3 %shard_map.51 = (f32[16,64,512]{2,1,0:T(8,128)}, f32[16,64,512]{2,1,0:T(8,128)}) custom-call(f32[16,64,512]{2,1,0:T(8,128)S(1)} %get-tuple-element.7.sol_ref, f32[16,64,512]{2,1,0:T(8,128)S(1)} %get-tuple-element.8.step_ref, f32[16,64,512]{2,1,0:T(8,128)S(1)} %get-tuple-element.9.res_ref, f32[16,64,512]{2,1,0:T(8,128)S(1)} %get-tuple-element.10.moved_ref, ...), custom_call_target="tpu_custom_call" | custom-call | tf_op jit(solution)/shard_map/pallas_call | solution.py:444

commit v2 on v1

--- a/solution.py
+++ b/solution.py
@@ -173,13 +173,16 @@
         A[stage] = row
         M[stage, me] = row
         for ox in range(px):
+            to_x = jnp.where(gx < px // 2, px - 1 - ox, ox)
             for oy in range(py):
-                if ox or oy:
+                to_y = jnp.where(gy < py // 2, py - 1 - oy, oy)
+
+                @pl.when(jnp.logical_or(to_x != gx, to_y != gy))
+                def _():
                     pltpu.make_async_remote_copy(
                         src_ref=A.at[stage], dst_ref=M.at[stage, me],
                         send_sem=as_sem.at[stage], recv_sem=ar_sem.at[stage],
-                        device_id={"gx": lax.rem(gx + ox, px), "gy": lax.rem(gy + oy, py)},
-                        device_id_type=MESH,
+                        device_id={"gx": to_x, "gy": to_y}, device_id_type=MESH,
                     ).start()
 
     def all_sums(stage):
@@ -246,7 +249,7 @@
 
     c_scale = 2.0 / half_range
 
-    def block(k, x, y, n):
+    def block(k, x, y, n, without=None):
         at, up, down = pl.ds(PAD + y, n), pl.ds(PAD + y + 1, n), pl.ds(PAD + y - 1, n)
         lane = lax.broadcasted_iota(jnp.int32, (n, 128), 1)
         first_lane, last_lane = lane == 0, lane == 127
@@ -255,7 +258,8 @@
         left = [pltpu.roll(h, 127, 1) for h in here]
         squares, crosses = [], []
         for z in range(ZC):
-            beside = F[k - 1, z, x + 1, at, :] + F[k - 1, z, x - 1, at, :]
+            inside = [p for p in (x + 1, x - 1) if without is None or p != without]
+            beside = total(F[k - 1, z, p, at, :] for p in inside)
             beside = beside + (F[k - 1, z, x, up, :] + F[k - 1, z, x, down, :])
             before = jnp.where(first_lane, right[z - 1] if z > 0 else 0.0, right[z])
             after = jnp.where(last_lane, left[z + 1] if z < ZC - 1 else 0.0, left[z])
@@ -269,10 +273,23 @@
             else:
                 new = diag * here[z] - beside * c_scale - F[k - 2, z, x, at, :]
             F[k, z, x, at, :] = new
+            if without is not None:
+                continue
             squares.append(fold(new * new))
             if k > 1:
                 crosses.append(fold(new * here[z]))
-        return total(squares), (total(crosses) if k > 1 else zero_tile)
+        if without is None:
+            return total(squares), (total(crosses) if k > 1 else zero_tile)
+
+    def complete(k, x, beyond, y, n):
+        at = pl.ds(PAD + y, n)
+        squares, crosses = [], []
+        for z in range(ZC):
+            new = F[k, z, x, at, :] - c_scale * F[k - 1, z, beyond, at, :]
+            F[k, z, x, at, :] = new
+            squares.append(fold(new * new))
+            crosses.append(fold(new * F[k - 1, z, x, at, :]))
+        return total(squares), total(crosses)
 
     def add(a, b):
         return a[0] + b[0], a[1] + b[1]
@@ -342,10 +359,14 @@
         return s
 
     sums = lax.fori_loop(2, LX, inner_plane, (zero_tile, zero_tile))
+    ends = ((1, 0), (LX, LX + 1))
+    for x, beyond in ends:
+        for j in order:
+            block(last, x, j * rows, rows, without=beyond)
     for j in order:
         wait_x(last - 1, j)
-        for x in (1, LX):
-            sums = add(sums, block(last, x, j * rows, rows))
+        for x, beyond in ends:
+            sums = add(sums, complete(last, x, beyond, j * rows, rows))
     send_sums(1, row_of([(2 * STEPS - 1, sums[1]), (2 * STEPS, sums[0])]))
 
     got = moments_of(0, early)
@@ -372,10 +393,6 @@
 
     lax.fori_loop(0, LX, plane, 0)
 
-    got.update(moments_of(1, late))
-    moments += [moment(m) for m in late]
-    alpha_out[...] = rr / quad(pc, gram_of(moments, STEPS + 1), moved)
-
     for k in range(STEPS + 1):
         for side in (0, 1):
             def done():
@@ -383,14 +400,19 @@
                     x_copy(k, side, j).wait_send()
             pl.when(x_has[side])(done)
             pl.when(y_has[side])(lambda: y_copy(k, side).wait_send())
-    for stage in (0, 1):
-        all_sums(stage).wait_send()
+    all_sums(0).wait_send()
+
+    got.update(moments_of(1, late))
+    moments += [moment(m) for m in late]
+    alpha_out[...] = rr / quad(pc, gram_of(moments, STEPS + 1), moved)
+
+    all_sums(1).wait_send()
 
 
 def last_step(sol_ref, step_ref, res_ref, moved_ref, alpha_ref, sol_hbm, res_hbm, sol, res, sems):
     LX, LY, LZ = sol.shape
     alpha = jnp.concatenate([alpha_ref[...]] * (LZ // 128), axis=1)
-    n = 2 if LX % 2 == 0 else 1
+    n = 1
     copies = []
     for x in range(0, LX, n):
         for i, (out, hbm) in enumerate(((sol, sol_hbm), (res, res_hbm))):

time: 44.5 us -> 44.3 us (level)
  no operation moved by 1% of the time
where the time goes in v2:
time: 44.3 us; the launch traced here: 44.2 us
  Pallas kernels  43.5 us (98%)
  between operations  0.64 us (1%)
    pallas_call x1, Pallas kernels, shards(): pl.pallas_call(functools.partial(kernel, px, py, rows), out_shape=(like,)...  41.2 us
    pallas_call x1, Pallas kernels, shards(): pl.pallas_call(last_step, out_shape=(like,) * 2, in_specs=[vmem] * 5, out...  2.28 us

profile of v2, /device:TPU:0, one launch (start us, length us, event | category | flops | bytes accessed | tf_op | source)
XLA Modules:
  0.0 44.2 jit_solution(7751352328071433303)
XLA Ops:
  0.6 41.2 %shard_map.50 = (f32[16,64,512]{2,1,0:T(8,128)S(1)}, f32[16,64,512]{2,1,0:T(8,128)S(1)}, f32[16,64,512]{2,1,0:T(8,128)S(1)}, f32[16,64,512]{2,1,0:T(8,128)S(1)}, f32[8,128]{1,0:T(8,128)S(1)}) custom-call(f32[16,64,512]{2,1,0:T(8,128)} %r_hbm.1, f32[16,64,512]{2,1,0:T(8,128)} %g_hbm.1, f32[16,64,512]{2,1,0:T(8,128)} %d_hbm.1), custom_call_target="tpu_custom_call" | custom-call | tf_op jit(solution)/shard_map/pallas_call | solution.py:444
  41.9 2.3 %shard_map.51 = (f32[16,64,512]{2,1,0:T(8,128)}, f32[16,64,512]{2,1,0:T(8,128)}) custom-call(f32[16,64,512]{2,1,0:T(8,128)S(1)} %get-tuple-element.7.sol_ref, f32[16,64,512]{2,1,0:T(8,128)S(1)} %get-tuple-element.8.step_ref, f32[16,64,512]{2,1,0:T(8,128)S(1)} %get-tuple-element.9.res_ref, f32[16,64,512]{2,1,0:T(8,128)S(1)} %get-tuple-element.10.moved_ref, ...), custom_call_target="tpu_custom_call" | custom-call | tf_op jit(solution)/shard_map/pallas_call | solution.py:466

commit v3 on v2

--- a/solution.py
+++ b/solution.py
@@ -214,12 +214,12 @@
             device_id_type=MESH,
         )
 
-    def send_x(k, j):
-        for side in (0, 1):
+    def send_x(k, j, sides=(0, 1)):
+        for side in sides:
             pl.when(x_has[side])(lambda: x_copy(k, side, j).start())
 
-    def wait_x(k, j):
-        for side in (0, 1):
+    def wait_x(k, j, sides=(0, 1)):
+        for side in sides:
             pl.when(x_has[1 - side])(lambda: x_copy(k, side, j).wait_recv())
 
     def send_y(k):
@@ -321,10 +321,10 @@
         sums = (zero_tile, zero_tile)
         wait_y(k - 1)
         for i, j in enumerate(order):
-            wait_x(k - 1, j)
-            for x in (1, LX):
+            for side, x in ((0, 1), (1, LX)):
+                wait_x(k - 1, j, (1 - side,))
                 sums = add(sums, block(k, x, j * rows, rows))
-            send_x(k, j)
+                send_x(k, j, (side,))
             if i == 1:
                 send_y(k)
             if i == 0:
@@ -364,8 +364,8 @@
         for j in order:
             block(last, x, j * rows, rows, without=beyond)
     for j in order:
-        wait_x(last - 1, j)
-        for x, beyond in ends:
+        for side, (x, beyond) in enumerate(ends):
+            wait_x(last - 1, j, (1 - side,))
             sums = add(sums, complete(last, x, beyond, j * rows, rows))
     send_sums(1, row_of([(2 * STEPS - 1, sums[1]), (2 * STEPS, sums[0])]))
 

time: 44.3 us -> 43.8 us (0.989)
    pallas_call x1, Pallas kernels: 41.2 us -> 40.8 us  [shards(): pl.pallas_call(functools.partial(kernel, px, py, rows), out_shape=(like,)...]
where the time goes in v3:
time: 43.8 us; the launch traced here: 43.7 us
  Pallas kernels  43.1 us (98%)
  between operations  0.64 us (1%)
    pallas_call x1, Pallas kernels, shards(): pl.pallas_call(functools.partial(kernel, px, py, rows), out_shape=(like,)...  40.8 us
    pallas_call x1, Pallas kernels, shards(): pl.pallas_call(last_step, out_shape=(like,) * 2, in_specs=[vmem] * 5, out...  2.28 us

profile of v3, /device:TPU:0, one launch (start us, length us, event | category | flops | bytes accessed | tf_op | source)
XLA Modules:
  0.0 43.7 jit_solution(11328315950286361518)
XLA Ops:
  0.6 40.8 %shard_map.50 = (f32[16,64,512]{2,1,0:T(8,128)S(1)}, f32[16,64,512]{2,1,0:T(8,128)S(1)}, f32[16,64,512]{2,1,0:T(8,128)S(1)}, f32[16,64,512]{2,1,0:T(8,128)S(1)}, f32[8,128]{1,0:T(8,128)S(1)}) custom-call(f32[16,64,512]{2,1,0:T(8,128)} %r_hbm.1, f32[16,64,512]{2,1,0:T(8,128)} %g_hbm.1, f32[16,64,512]{2,1,0:T(8,128)} %d_hbm.1), custom_call_target="tpu_custom_call" | custom-call | tf_op jit(solution)/shard_map/pallas_call | solution.py:444
  41.4 2.3 %shard_map.51 = (f32[16,64,512]{2,1,0:T(8,128)}, f32[16,64,512]{2,1,0:T(8,128)}) custom-call(f32[16,64,512]{2,1,0:T(8,128)S(1)} %get-tuple-element.7.sol_ref, f32[16,64,512]{2,1,0:T(8,128)S(1)} %get-tuple-element.8.step_ref, f32[16,64,512]{2,1,0:T(8,128)S(1)} %get-tuple-element.9.res_ref, f32[16,64,512]{2,1,0:T(8,128)S(1)} %get-tuple-element.10.moved_ref, ...), custom_call_target="tpu_custom_call" | custom-call | tf_op jit(solution)/shard_map/pallas_call | solution.py:466
